TPU v7x, 32 devices: a whole 2x2x4 slice. The times are simulated.
32 devices in a mesh: grp: 2 (over y), seq: 4 (over z), head: 2 (over x), rep: 2 (over core).
Axes of the slice: x: 2, y: 2, z: 4, core: 2. Of those that a mesh axis runs over, the one named last changes fastest.
Arguments:
- queries: bfloat16 [32, 64, 128], P(('grp', 'rep'), 'head'), parts along dimension 0, may hold values from -16 to 16
- key_cache: bfloat16 [32, 4, 2048, 128], P(('grp', 'rep'), 'head', 'seq'), parts along dimension 0, may hold values from -7 to 7
- value_cache: bfloat16 [32, 4, 2048, 128], P(('grp', 'rep'), 'head', 'seq'), parts along dimension 0, may hold values from -6 to 6
- indices: int32 [32, 4, 16], P(('grp', 'rep'), 'head'), parts along dimension 0, may hold values from 0 to 31, as said below
- counts: int32 [32, 4], P(('grp', 'rep'), 'head'), parts along dimension 0, may hold values from 8 to 16, as said below
- lengths: int32 [32], P(('grp', 'rep')), parts along dimension 0, may hold values from 1024 to 2048
Outputs:
- attended: bfloat16 [32, 64, 128], P(('grp', 'rep'), 'head', 'seq'), parts along dimension 0
There are 2 independent parts, one for each index of `grp`. A program takes and returns all parts, laid end to end along the dimension named above; each array names one. Nothing has to cross between parts.
Inputs may be any that keep to these rules, and one draw needn't show every extreme that they name: `indices`: within a row and key-value head the 16 blocks are distinct, and each holds at least one token below the row's length. `counts`: some row uses all 16 slots.
All inputs are finite; a program needn't handle non-finite values.
Results may differ from a plain program's by a relative error of at most 0.0015.
Values sent between devices are 32-bit elements; how exact they have to be, the bound alone decides.
No kernel may reach another device: no remote copies, remote signals or barrier semaphores. Data moves between devices by JAX's collectives and lax.ppermute only.
A program may use at most 64 MiB of HBM per device.

v0:
```python
import jax
import jax.numpy as jnp
from jax import lax
from jax.sharding import PartitionSpec as P

BLOCK = 64
SLOTS = 16


lowest = -1e30


def joined(value, axis, join):
    pieces = jax.tree.map(lambda part: lax.all_gather(part, axis), value)
    head = jax.tree.map(lambda part: part[0], pieces)
    tail = jax.tree.map(lambda part: part[1:], pieces)
    subtotal, _ = lax.scan(lambda subtotal, section: (join(subtotal, section), None), head, tail)
    return subtotal


def join_partials(first, second):
    first_running_max, first_total, first_summed = first
    second_running_max, second_total, second_summed = second
    highest = jnp.maximum(first_running_max, second_running_max)
    first_factor = jnp.exp(first_running_max - highest)
    second_factor = jnp.exp(second_running_max - highest)
    total = first_total * first_factor + second_total * second_factor
    weighted_value_sum = (
        first_summed * first_factor[..., None] + second_summed * second_factor[..., None]
    )
    return (highest, total, weighted_value_sum)


def local(queries, key_cache, value_cache, indices, counts, lengths):
    batch_rows, heads_local, ctx_local, key_width = key_cache.shape
    value_width = value_cache.shape[3]
    group = queries.shape[1] // heads_local
    rescale_factor = key_width ** (-0.5)
    seq_index = lax.axis_index("seq")
    seq_count = lax.axis_size("seq")
    query_grouped = queries.reshape(batch_rows, heads_local, group, key_width)
    slot_used = jnp.arange(SLOTS, dtype=jnp.int32)[None, None, :] < counts[:, :, None]
    position = seq_index * ctx_local + jnp.arange(ctx_local, dtype=jnp.int32)
    block_number = position // BLOCK
    matches = (indices[:, :, :, None] == block_number[None, None, None, :]) & slot_used[
        :, :, :, None
    ]
    picked = jnp.any(matches, axis=2)
    live = picked & (position[None, None, :] < lengths[:, None, None])
    scores = (
        jnp.einsum("bhgd,bhkd->bhgk", query_grouped, key_cache, preferred_element_type=jnp.float32)
        * rescale_factor
    )
    scores = jnp.where(live[:, :, None, :], scores, -jnp.inf)
    local_top = jnp.maximum(jnp.max(scores, axis=-1), lowest)
    softmax_weights = jnp.exp(scores - local_top[..., None])
    local_total = jnp.sum(softmax_weights, axis=-1)
    local_summed = jnp.einsum(
        "bhgk,bhkv->bhgv",
        softmax_weights,
        value_cache.astype(jnp.float32),
        precision=lax.Precision.HIGHEST,
    )
    share_width = value_width // seq_count
    highest, total, weighted_value_sum = joined(
        (local_top, local_total, local_summed), "seq", join_partials
    )
    result = (weighted_value_sum / total[..., None]).reshape(
        batch_rows, heads_local * group, value_width
    )
    result = lax.dynamic_slice_in_dim(result, seq_index * share_width, share_width, 2)
    return result.astype(jnp.bfloat16)


def solution(mesh):
    return jax.shard_map(
        local,
        mesh=mesh,
        in_specs=(
            P(("grp", "rep"), "head", None),
            P(("grp", "rep"), "head", "seq", None),
            P(("grp", "rep"), "head", "seq", None),
            P(("grp", "rep"), "head", None),
            P(("grp", "rep"), "head"),
            P(("grp", "rep")),
        ),
        out_specs=P(("grp", "rep"), "head", "seq"),
        check_vma=False,
    )
```

profile of v0, /device:TPU:0, one launch (start us, length us, event | category | flops | bytes accessed | tf_op | source)
XLA Modules:
  0.0 50.9 jit_solution(10579788579333582362)
XLA Ops:
  0.0 0.0 copy-start
  0.0 0.9 %broadcast_compare_fusion = pred[8,512]{1,0:T(8,128)(4,1)S(1)} fusion(s32[512]{0:T(512)S(1)} %get-tuple-element.66, s32[8]{0:T(128)} %param.13), kind=kLoop, calls=%fused_computation.18 | loop fusion | flops 4096 | bytes 6176 | tf_op jit(solution)/shard_map/lt | solution.py:49
  0.9 0.8 %copy.9 = s32[8,2]{1,0:T(8,128)S(1)} copy(s32[8,2]{0,1:T(2,128)} %param.12) | data formatting | bytes 128 | tf_op args[4]
  1.6 0.0 copy-start.1
  1.6 0.1 iota_compare_fusion
  1.7 1.1 %and_reduce_fusion = pred[8,2,512]{2,1,0:T(4,128)(4,1)S(1)} fusion(s32[512]{0:T(512)S(1)} %get-tuple-element.65, s32[8,2,16]{2,1,0:T(2,128)} %param.11, pred[8,2,16]{2,1,0:T(4,128)(4,1)S(1)} %iota_compare_fusion), kind=kLoop, calls=%fused_computation.11 | loop fusion | flops 385024 | bytes 11520 | tf_op jit(solution)/shard_map/reduce_or | solution.py:48
  2.8 0.0 copy-done
  2.8 1.6 %fusion.11 = (f32[8,2,16]{2,1,0:T(2,128)S(1)}, f32[8,2,16,512]{3,2,1,0:T(8,128)S(1)}) fusion(bf16[8,2,16,128]{3,2,1,0:T(8,128)(2,1)} %bitcast.31, bf16[8,2,512,128]{3,2,1,0:T(8,128)(2,1)S(1)} %copy-done, pred[8,2,512]{2,1,0:T(4,128)(4,1)S(1)} %broadcast_and_fusion), kind=kOutput, calls=%fused_computation.30 | convolution fusion | flops 33947392 | bytes 2696192 | tf_op jit(solution)/shard_map/bhgd,bhkd->bhgk/dot_general | solution.py:51
  4.4 0.3 fusion.5
  4.7 0.0 copy-done.1
  4.7 1.0 %fusion.4 = f32[8,2,16,128]{3,2,1,0:T(8,128)S(1)} fusion(bf16[8,2,512,128]{3,2,1,0:T(8,128)(2,1)S(1)} %copy-done.1, f32[8,2,16,512]{3,2,1,0:T(8,128)S(1)} %get-tuple-element.64, f32[8,2,16]{2,1,0:T(2,128)S(1)} %broadcast_maximum_fusion), kind=kOutput, calls=%fused_computation.12 | convolution fusion | flops 201457664 | bytes 2753536 | tf_op jit(solution)/shard_map/bhgk,bhkv->bhgv/dot_general | solution.py:58
  5.7 14.8 %all-gather = f32[32,2,16]{2,1,0:T(2,128)S(1)} all-gather(f32[8,2,16]{2,1,0:T(2,128)S(1)} %broadcast_maximum_fusion), channel_id=2, replica_groups=mesh['grp'=2,'seq'=4,'head'=2,'rep'=2] {'seq'}, dimensions={0}, use_global_device_ids=true | all-gather | bytes 5120 | tf_op jit(solution)/shard_map/all_gather | solution.py:14
  20.6 13.1 %all-gather.1 = f32[32,2,16]{2,1,0:T(2,128)S(1)} all-gather(f32[8,2,16]{2,1,0:T(2,128)S(1)} %fusion.5), channel_id=3, replica_groups=mesh['grp'=2,'seq'=4,'head'=2,'rep'=2] {'seq'}, dimensions={0}, use_global_device_ids=true | all-gather | bytes 5120 | tf_op jit(solution)/shard_map/all_gather | solution.py:14
  33.7 15.7 %all-gather.2 = f32[32,2,16,128]{3,2,1,0:T(8,128)S(1)} all-gather(f32[8,2,16,128]{3,2,1,0:T(8,128)S(1)} %fusion.4), channel_id=4, replica_groups=mesh['grp'=2,'seq'=4,'head'=2,'rep'=2] {'seq'}, dimensions={0}, use_global_device_ids=true | all-gather | bytes 655360 | tf_op jit(solution)/shard_map/all_gather | solution.py:14
  49.4 0.7 %while.14 = (s32[]{:T(128)}, f32[8,2,16]{2,1,0:T(2,128)S(1)}, f32[8,2,16]{2,1,0:T(2,128)S(1)}, f32[8,2,16,128]{3,2,1,0:T(8,128)S(1)}, f32[3,8,2,16]{3,2,1,0:T(2,...) while((s32[]{:T(128)}, f32[8,2,16]{2,1,0:T(2,128)S(1)}, ...), condition=%wide.region_4.5_spmd, body=%wide.region_3.4_spmd.sunk | while | flops 99842 | bytes 403557 | solution.py:17
  49.5 0.2 fusion.18
  49.7 0.2 fusion.18
  49.9 0.2 fusion.18
  50.1 0.1 broadcast_divide_fusion
  50.2 0.7 %dynamic-slice_convert_fusion = bf16[8,32,32]{2,1,0:T(8,128)(2,1)} fusion(bf16[8,32,128]{2,1,0:T(8,128)(2,1)S(1)} %bitcast.28, s32[]{:T(128)S(6)} %select_n.18), kind=kLoop, calls=%fused_computation.15 | loop fusion | bytes 32772 | tf_op jit(solution)/shard_map/convert_element_type | solution.py:72
  (12 shorter events, 0.2 us)
Async XLA Ops:
  0.0 2.8 %copy-start = (bf16[8,2,512,128]{3,2,1,0:T(8,128)(2,1)S(1)}, bf16[8,2,512,128]{3,2,1,0:T(8,128)(2,1)}, u32[]{:S(2)}) copy-start(bf16[8,2,512,128]{3,2,1,0:T(8,128)(2,1)} %param.9) | copy-start | bytes 6291460
  1.6 3.0 %copy-start.1 = (bf16[8,2,512,128]{3,2,1,0:T(8,128)(2,1)S(1)}, bf16[8,2,512,128]{3,2,1,0:T(8,128)(2,1)}, u32[]{:S(2)}) copy-start(bf16[8,2,512,128]{3,2,1,0:T(8,128)(2,1)} %param.10) | copy-start | bytes 6291460
where the time goes:
time: 51.2 us; the launch traced here: 50.9 us
  blocking collectives  43.6 us (85%)
  other arithmetic  3.04 us (6%)
  matrix products  2.59 us (5%)
  local copies, waits for them, and re-layouts  1.53 us (3%)
    all_gather x3, blocking collectives, joined(): pieces = jax.tree.map(lambda part: lax.all_gather(part, axis), value)  43.6 us
    dot_general x1, matrix products, local(): jnp.einsum('bhgd,bhkd->bhgk', query_grouped, key_cache, preferred_element...  1.58 us
    reduce_or x1, other arithmetic, local(): picked = jnp.any(matches, axis=2)  1.06 us

commit v1 on v0

v1 whole, which is shorter than its diff:
```python
import functools

import jax
import jax.numpy as jnp
from jax import lax
from jax.experimental import pallas as pl
from jax.experimental.pallas import tpu as pltpu
from jax.sharding import PartitionSpec as P

BLOCK = 64
LANES = 128
SUBLANES = 8
LOG2E = 1.4426950408889634

lowest = -1e30
masked = -2e30


def partial_kernel(
    seq_count,
    relative,
    queries_hbm,
    keys_hbm,
    values_hbm,
    indices_hbm,
    counts_hbm,
    lengths_hbm,
    *refs,
):
    outs = refs[: seq_count if relative else 1]
    (
        queries,
        keys,
        values,
        indices,
        counts,
        lengths,
        weights,
        summed,
        flipped,
        small_sems,
        key_sems,
        value_sems,
    ) = refs[len(outs) :]
    batch_rows, heads_local, ctx_local, key_width = keys_hbm.shape
    value_width = values_hbm.shape[3]
    group = queries_hbm.shape[1] // heads_local
    slots = indices_hbm.shape[2]
    pairs = [(b, h) for b in range(batch_rows) for h in range(heads_local)]
    share = value_width // seq_count
    seq_index = lax.axis_index("seq")

    small = [
        pltpu.make_async_copy(src, dst, small_sems.at[n])
        for n, (src, dst) in enumerate(
            (
                (indices_hbm, indices),
                (counts_hbm, counts),
                (lengths_hbm, lengths),
                (queries_hbm, queries),
            )
        )
    ]
    for copy in small:
        copy.start()
    key_copies = [
        pltpu.make_async_copy(keys_hbm.at[b, h], keys.at[n], key_sems.at[n])
        for n, (b, h) in enumerate(pairs)
    ]
    value_copies = [
        pltpu.make_async_copy(values_hbm.at[b, h], values.at[n], value_sems.at[n])
        for n, (b, h) in enumerate(pairs)
    ]
    for copy in key_copies:
        copy.start()
    for copy in value_copies:
        copy.start()
    for copy in small:
        copy.wait()

    blocks = ctx_local // BLOCK
    base = seq_index * blocks
    slot = lax.broadcasted_iota(jnp.int32, (1, slots), 1)
    lane = lax.broadcasted_iota(jnp.int32, (1, ctx_local), 1)
    lane_block = lane // BLOCK
    position = lane + seq_index * ctx_local
    scale = LOG2E * key_width ** (-0.5)

    per_tile = LANES // group
    tiles = len(pairs) // per_tile
    row = lax.broadcasted_iota(jnp.int32, (group, LANES), 0)
    column = lax.broadcasted_iota(jnp.int32, (group, LANES), 1)
    tops = [jnp.zeros((group, LANES), jnp.float32) for _ in range(tiles)]
    totals = [jnp.zeros((group, LANES), jnp.float32) for _ in range(tiles)]
    for n, (b, h) in enumerate(pairs):
        offset = indices[b, h : h + 1, :] - base
        used = (slot < counts[h, b]) & (offset >= 0) & (offset < blocks)
        bits = jnp.sum(jnp.where(used, 1 << (offset & 31), 0), axis=1, keepdims=True)
        live = (((bits >> lane_block) & 1) != 0) & (position < lengths[b])
        key_copies[n].wait()
        scores = lax.dot_general(
            queries[b, h * group : (h + 1) * group, :],
            keys[n],
            (((1,), (1,)), ((), ())),
            preferred_element_type=jnp.float32,
        )
        scores = jnp.where(live, scores * scale, masked)
        top = jnp.maximum(jnp.max(scores, axis=1, keepdims=True), lowest)
        softmax_weights = jnp.exp2(scores - top)
        total = jnp.sum(softmax_weights, axis=1, keepdims=True)
        high = softmax_weights.astype(jnp.bfloat16)
        low = (softmax_weights - high.astype(jnp.float32)).astype(jnp.bfloat16)
        weights[n, :group] = high
        weights[n, group:] = low
        tile = n // per_tile
        mine = column == row + (n % per_tile) * group
        tops[tile] = jnp.where(mine, top, tops[tile])
        totals[tile] = jnp.where(mine, total, totals[tile])
    for n in range(len(pairs)):
        value_copies[n].wait()
        both = lax.dot_general(
            weights[n],
            values[n],
            (((1,), (0,)), ((), ())),
            preferred_element_type=jnp.float32,
        )
        summed[n * group : (n + 1) * group, :] = both[:group] + both[group:]

    stats = jnp.zeros((SUBLANES, LANES), jnp.float32)
    line = lax.broadcasted_iota(jnp.int32, (SUBLANES, LANES), 0)
    for tile in range(tiles):
        stats = jnp.where(line == tile, jnp.sum(tops[tile], axis=0, keepdims=True), stats)
        stats = jnp.where(line == tiles + tile, jnp.sum(totals[tile], axis=0, keepdims=True), stats)
        flipped[tile] = summed[tile * LANES : (tile + 1) * LANES, :].T

    for s in range(seq_count):
        if relative:
            out = outs[s]
            start = pl.multiple_of((seq_index ^ s) * share, share)
            for tile in range(tiles):
                out[tile * share : (tile + 1) * share] = flipped[tile, pl.ds(start, share), :]
            out[tiles * share :] = stats
        else:
            for tile in range(tiles):
                outs[0][s, tile * share : (tile + 1) * share] = flipped[
                    tile, s * share : (s + 1) * share, :
                ]
            outs[0][s, outs[0].shape[1] - SUBLANES :] = stats


def join_kernel(tiles, share, group, *refs):
    *pieces, out = refs
    if len(pieces) == 1:
        pieces = [pieces[0].at[s] for s in range(pieces[0].shape[0])]
    stats = [piece[piece.shape[0] - SUBLANES :] for piece in pieces]
    batch_rows = out.shape[0]
    per_row = out.shape[1]
    rows_of_tile = LANES // per_row
    for tile in range(tiles):
        tops = [stat[tile : tile + 1] for stat in stats]
        highest = functools.reduce(jnp.maximum, tops)
        factors = [jnp.exp2(top - highest) for top in tops]
        total = sum(
            factor * stat[tiles + tile : tiles + tile + 1]
            for factor, stat in zip(factors, stats, strict=True)
        )
        weighted = sum(
            factor * piece[tile * share : (tile + 1) * share]
            for factor, piece in zip(factors, pieces, strict=True)
        )
        result = (weighted / total).T
        out[tile * rows_of_tile : (tile + 1) * rows_of_tile] = result.reshape(
            rows_of_tile, per_row, share
        ).astype(out.dtype)


def local(queries, key_cache, value_cache, indices, counts, lengths):
    batch_rows, heads_local, ctx_local, key_width = key_cache.shape
    value_width = value_cache.shape[3]
    heads = queries.shape[1]
    group = heads // heads_local
    seq_count = lax.axis_size("seq")
    share = value_width // seq_count
    pairs = batch_rows * heads_local
    tiles = pairs * group // LANES
    piece_rows = -(-tiles * share // SUBLANES) * SUBLANES + SUBLANES
    relative = seq_count in (2, 4, 8)
    any_space = pl.BlockSpec(memory_space=pltpu.HBM)
    vmem = pl.BlockSpec(memory_space=pltpu.VMEM)
    if relative:
        out_shape = [jax.ShapeDtypeStruct((piece_rows, LANES), jnp.float32)] * seq_count
    else:
        out_shape = [jax.ShapeDtypeStruct((seq_count, piece_rows, LANES), jnp.float32)]
    pieces = pl.pallas_call(
        functools.partial(partial_kernel, seq_count, relative),
        out_shape=out_shape,
        in_specs=[any_space] * 6,
        out_specs=[vmem] * len(out_shape),
        scratch_shapes=[
            pltpu.VMEM(queries.shape, queries.dtype),
            pltpu.VMEM((pairs, ctx_local, key_width), key_cache.dtype),
            pltpu.VMEM((pairs, ctx_local, value_width), value_cache.dtype),
            pltpu.VMEM(indices.shape, indices.dtype),
            pltpu.SMEM((heads_local, batch_rows), counts.dtype),
            pltpu.SMEM(lengths.shape, lengths.dtype),
            pltpu.VMEM((pairs, 2 * group, ctx_local), jnp.bfloat16),
            pltpu.VMEM((pairs * group, value_width), jnp.float32),
            pltpu.VMEM((tiles, value_width, LANES), jnp.float32),
            pltpu.SemaphoreType.DMA((4,)),
            pltpu.SemaphoreType.DMA((pairs,)),
            pltpu.SemaphoreType.DMA((pairs,)),
        ],
        name="partial_attention",
    )(queries, key_cache, value_cache, indices, counts.T, lengths)
    if relative:
        arrived = [pieces[0]] + [
            lax.ppermute(pieces[s], "seq", [(i, i ^ s) for i in range(seq_count)])
            for s in range(seq_count - 1, 0, -1)
        ]
    else:
        arrived = [lax.all_to_all(pieces[0], "seq", 0, 0)]
    return pl.pallas_call(
        functools.partial(join_kernel, tiles, share, group),
        out_shape=jax.ShapeDtypeStruct((batch_rows, heads, share), jnp.bfloat16),
        in_specs=[vmem] * len(arrived),
        out_specs=vmem,
        name="join_partials",
    )(*arrived)


def solution(mesh):
    return jax.shard_map(
        local,
        mesh=mesh,
        in_specs=(
            P(("grp", "rep"), "head", None),
            P(("grp", "rep"), "head", "seq", None),
            P(("grp", "rep"), "head", "seq", None),
            P(("grp", "rep"), "head", None),
            P(("grp", "rep"), "head"),
            P(("grp", "rep")),
        ),
        out_specs=P(("grp", "rep"), "head", "seq"),
        check_vma=False,
    )
```

time: 51.2 us -> 23.2 us (0.45)
  blocking collectives: 43.6 us -> 0 us
  Pallas kernels: 0 us -> 12.2 us
  starting transfers between devices: 0 us -> 5.79 us
  waiting for transfers between devices: 0 us -> 4.43 us
  other arithmetic: 3.04 us -> 0 us
  matrix products: 2.59 us -> 0 us
  local copies, waits for them, and re-layouts: 1.53 us -> 0.62 us
    all_gather x3 -> x0, blocking collectives: 43.6 us -> none  [joined(): pieces = jax.tree.map(lambda part: lax.all_gather(part, axis), value)]
    pallas_call x0 -> x2, Pallas kernels: none -> 12.2 us  [the longest x1 10.6 us: local(): pl.pallas_call(functools.partial(partial_kernel, seq_count, relative), ou...]
    ppermute x0 -> x3, starting transfers between devices: none -> 5.79 us  [local(): lax.ppermute(pieces[s], 'seq', [(i, i ^ s) for i in range(seq_count)])]
    ppermute x0 -> x3, waiting for transfers between devices: none -> 4.43 us  [local(): lax.ppermute(pieces[s], 'seq', [(i, i ^ s) for i in range(seq_count)])]
    dot_general x2 -> x0, matrix products: 2.59 us -> none  [the longest x1 1.58 us: local(): jnp.einsum('bhgd,bhkd->bhgk', query_grouped, key_cache, preferred_element...]
    reduce_or x1 -> x0, other arithmetic: 1.06 us -> none  [local(): picked = jnp.any(matches, axis=2)]
    lt x2 -> x0, other arithmetic: 0.95 us -> none  [the longest x1 0.88 us: local(): live = picked & (position[None, None, :] < lengths[:, None, None])]
    convert_element_type x1 -> x0, local copies, waits for them, and re-layouts: 0.72 us -> none  [local(): return result.astype(jnp.bfloat16)]
  transfers between devices with their start and end apart: 0 -> 3, of which waited for: 0 -> 2; matrix products, arithmetic and copies ran while one was open for 0% -> 0% of each run, Pallas kernels for 0% -> 0%
where the time goes in v1:
time: 23.2 us; the launch traced here: 23 us
  Pallas kernels  12.2 us (53%)
  starting transfers between devices  5.79 us (25%)
  waiting for transfers between devices  4.43 us (19%)
  local copies, waits for them, and re-layouts  0.62 us (3%)
    pallas_call x1, Pallas kernels, local(): pl.pallas_call(functools.partial(partial_kernel, seq_count, relative), ou...  10.6 us
    ppermute x3, starting transfers between devices, local(): lax.ppermute(pieces[s], 'seq', [(i, i ^ s) for i in range(seq_count)])  5.79 us
    ppermute x3, waiting for transfers between devices, local(): lax.ppermute(pieces[s], 'seq', [(i, i ^ s) for i in range(seq_count)])  4.43 us
    pallas_call x1, Pallas kernels, local(): pl.pallas_call(functools.partial(join_kernel, tiles, share, group), out_s...  1.58 us
    unnamed x6, local copies, waits for them, and re-layouts  0.62 us
  transfers between devices with their start and end apart: 3, of which 2 were waited for; matrix products, arithmetic and copies ran while one was open for 0% of the time, Pallas kernels for 0%

profile of v1, /device:TPU:0, one launch (start us, length us, event | category | flops | bytes accessed | tf_op | source)
XLA Modules:
  0.0 23.0 jit_solution(14625636146898919470)
XLA Ops:
  0.0 10.6 %partial_attention.1 = (f32[72,128]{1,0:T(8,128)}, f32[72,128]{1,0:T(8,128)}, f32[72,128]{1,0:T(8,128)}, f32[72,128]{1,0:T(8,128)}) custom-call(bf16[8,32,128]{2,1,0:T(8,128)(2,1)} %queries_hbm.1, bf16[8,2,512,128]{3,2,1,0:T(8,128)(2,1)} %keys_hbm.1, bf16[8,2,512,128]{3,2,1,0:T(8,128)(2,1)} %values_hbm.1, s32[8,2,16]{2,1,0:T(2,128)} %indices_hbm.1, ...), custom_call_target="tpu_custom_call" | custom-call | tf_op jit(solution)/shard_map/partial_attention/pallas_call | solution.py:194
  10.6 5.1 %collective-permute-start = (f32[72,128]{1,0:T(8,128)}, f32[72,128]{1,0:T(8,128)S(1)}, u32[]{:S(2)}, u32[]{:S(2)}) collective-permute-start(f32[72,128]{1,0:T(8,128)} %get-tuple-element.10), channel_id=1, source_target_pairs={{0,12},{4,8},{8,4},{12,0},{1,13},{5,9},{9,5},{13,1},{2,14},{6,10},... | collective-permute-start | bytes 110600 | tf_op jit(solution)/shard_map/ppermute | solution.py:217
  15.7 0.0 collective-permute-start.1
  15.7 0.6 %collective-permute-start.2 = (f32[72,128]{1,0:T(8,128)}, f32[72,128]{1,0:T(8,128)S(1)}, u32[]{:S(2)}, u32[]{:S(2)}) collective-permute-start(f32[72,128]{1,0:T(8,128)} %get-tuple-element.12), channel_id=1, source_target_pairs={{0,4},{4,0},{8,12},{12,8},{1,5},{5,1},{9,13},{13,9},{2,6},{6,2},{1... | collective-permute-start | bytes 110600 | tf_op jit(solution)/shard_map/ppermute | solution.py:217
  16.4 1.5 %collective-permute-done.refs_1_ = f32[72,128]{1,0:T(8,128)S(1)} collective-permute-done((f32[72,128]{1,0:T(8,128)}, f32[72,128]{1,0:T(8,128)S(1)}, u32[]{:S(2)}, u32[]{:S(2)}) %collective-permute-start) | collective-permute-done | bytes 36896 | tf_op jit(solution)/shard_map/ppermute | solution.py:217
  17.9 0.0 copy-start
  17.9 2.9 %collective-permute-done.1.refs_2_ = f32[72,128]{1,0:T(8,128)S(1)} collective-permute-done((f32[72,128]{1,0:T(8,128)}, f32[72,128]{1,0:T(8,128)S(1)}, u32[]{:S(2)}, u32[]{:S(2)}) %collective-permute-start.1) | collective-permute-done | bytes 36896 | tf_op jit(solution)/shard_map/ppermute | solution.py:217
  20.8 0.0 copy-start.1
  20.8 0.0 collective-permute-done.2.refs_3_
  20.8 0.0 copy-start.2
  20.8 0.0 copy-done
  20.8 0.6 %copy-done.1 = f32[72,128]{1,0:T(8,128)} copy-done((f32[72,128]{1,0:T(8,128)}, f32[72,128]{1,0:T(8,128)S(1)}, u32[]{:S(2)}) %copy-start.1) | copy-done | bytes 36888
  21.4 0.0 copy-done.2
  21.4 1.6 %join_partials.1 = bf16[8,32,32]{2,1,0:T(8,128)(2,1)} custom-call(f32[72,128]{1,0:T(8,128)} %get-tuple-element.9.refs_0_, f32[72,128]{1,0:T(8,128)} %copy-done, f32[72,128]{1,0:T(8,128)} %copy-done.1, f32[72,128]{1,0:T(8,128)} %copy-done.2), custom_call_target="tpu_custom_call" | custom-call | tf_op jit(solution)/shard_map/join_partials/pallas_call | solution.py:222
Async XLA Ops:
  10.6 7.3 %collective-permute-start = (f32[72,128]{1,0:T(8,128)}, f32[72,128]{1,0:T(8,128)S(1)}, u32[]{:S(2)}, u32[]{:S(2)}) collective-permute-start(f32[72,128]{1,0:T(8,128)} %get-tuple-element.10), channel_id=1, source_target_pairs={{0,12},{4,8},{8,4},{12,0},{1,13},{5,9},{9,5},{13,1},{2,14},{6,10},... | collective-permute-start | bytes 110600 | tf_op jit(solution)/shard_map/ppermute | solution.py:217
  15.7 5.1 %collective-permute-start.1 = (f32[72,128]{1,0:T(8,128)}, f32[72,128]{1,0:T(8,128)S(1)}, u32[]{:S(2)}, u32[]{:S(2)}) collective-permute-start(f32[72,128]{1,0:T(8,128)} %get-tuple-element.11), channel_id=1, source_target_pairs={{0,8},{4,12},{8,0},{12,4},{1,9},{5,13},{9,1},{13,5},{2,10},{6,14},... | collective-permute-start | bytes 110600 | tf_op jit(solution)/shard_map/ppermute | solution.py:217
  15.7 5.1 %collective-permute-start.2 = (f32[72,128]{1,0:T(8,128)}, f32[72,128]{1,0:T(8,128)S(1)}, u32[]{:S(2)}, u32[]{:S(2)}) collective-permute-start(f32[72,128]{1,0:T(8,128)} %get-tuple-element.12), channel_id=1, source_target_pairs={{0,4},{4,0},{8,12},{12,8},{1,5},{5,1},{9,13},{13,9},{2,6},{6,2},{1... | collective-permute-start | bytes 110600 | tf_op jit(solution)/shard_map/ppermute | solution.py:217
  17.9 2.9 %copy-start = (f32[72,128]{1,0:T(8,128)}, f32[72,128]{1,0:T(8,128)S(1)}, u32[]{:S(2)}) copy-start(f32[72,128]{1,0:T(8,128)S(1)} %collective-permute-done.refs_1_) | copy-start | bytes 110596
  20.8 0.6 %copy-start.1 = (f32[72,128]{1,0:T(8,128)}, f32[72,128]{1,0:T(8,128)S(1)}, u32[]{:S(2)}) copy-start(f32[72,128]{1,0:T(8,128)S(1)} %collective-permute-done.1.refs_2_) | copy-start | bytes 110596
  20.8 0.6 %copy-start.2 = (f32[72,128]{1,0:T(8,128)}, f32[72,128]{1,0:T(8,128)S(1)}, u32[]{:S(2)}) copy-start(f32[72,128]{1,0:T(8,128)S(1)} %collective-permute-done.2.refs_3_) | copy-start | bytes 110596

commit v2 on v1

--- a/solution.py
+++ b/solution.py
@@ -10,6 +10,8 @@
 BLOCK = 64
 LANES = 128
 SUBLANES = 8
+CHUNKS = 1
+LAG = 1
 LOG2E = 1.4426950408889634
 
 lowest = -1e30
@@ -35,8 +37,6 @@
         indices,
         counts,
         lengths,
-        weights,
-        summed,
         flipped,
         small_sems,
         key_sems,
@@ -46,8 +46,9 @@
     value_width = values_hbm.shape[3]
     group = queries_hbm.shape[1] // heads_local
     slots = indices_hbm.shape[2]
-    pairs = [(b, h) for b in range(batch_rows) for h in range(heads_local)]
     share = value_width // seq_count
+    chunks = key_sems.shape[0]
+    rows = batch_rows // chunks
     seq_index = lax.axis_index("seq")
 
     small = [
@@ -61,20 +62,29 @@
             )
         )
     ]
+
+    def pieces_of(chunk, src, dst, sems):
+        return [
+            pltpu.make_async_copy(src.at[b, h], dst.at[b, h], sems.at[chunk])
+            for b in range(chunk * rows, (chunk + 1) * rows)
+            for h in range(heads_local)
+        ]
+
+    def whole_of(chunk, src, dst, sems):
+        part = pl.ds(chunk * rows, rows)
+        return pltpu.make_async_copy(src.at[part], dst.at[part], sems.at[chunk])
+
+    key_side = (keys_hbm, keys, key_sems)
+    value_side = (values_hbm, values, value_sems)
     for copy in small:
         copy.start()
-    key_copies = [
-        pltpu.make_async_copy(keys_hbm.at[b, h], keys.at[n], key_sems.at[n])
-        for n, (b, h) in enumerate(pairs)
-    ]
-    value_copies = [
-        pltpu.make_async_copy(values_hbm.at[b, h], values.at[n], value_sems.at[n])
-        for n, (b, h) in enumerate(pairs)
-    ]
-    for copy in key_copies:
-        copy.start()
-    for copy in value_copies:
-        copy.start()
+    for step in range(chunks + LAG):
+        if step < chunks:
+            for copy in pieces_of(step, *key_side):
+                copy.start()
+        if step >= LAG:
+            for copy in pieces_of(step - LAG, *value_side):
+                copy.start()
     for copy in small:
         copy.wait()
 
@@ -86,52 +96,77 @@
     position = lane + seq_index * ctx_local
     scale = LOG2E * key_width ** (-0.5)
 
-    per_tile = LANES // group
-    tiles = len(pairs) // per_tile
-    row = lax.broadcasted_iota(jnp.int32, (group, LANES), 0)
-    column = lax.broadcasted_iota(jnp.int32, (group, LANES), 1)
-    tops = [jnp.zeros((group, LANES), jnp.float32) for _ in range(tiles)]
-    totals = [jnp.zeros((group, LANES), jnp.float32) for _ in range(tiles)]
-    for n, (b, h) in enumerate(pairs):
+    def live_of(b, h):
         offset = indices[b, h : h + 1, :] - base
         used = (slot < counts[h, b]) & (offset >= 0) & (offset < blocks)
         bits = jnp.sum(jnp.where(used, 1 << (offset & 31), 0), axis=1, keepdims=True)
-        live = (((bits >> lane_block) & 1) != 0) & (position < lengths[b])
-        key_copies[n].wait()
-        scores = lax.dot_general(
+        return (((bits >> lane_block) & 1) != 0) & (position < lengths[b])
+
+    def scores_of(b, h):
+        return lax.dot_general(
             queries[b, h * group : (h + 1) * group, :],
-            keys[n],
+            keys[b, h],
             (((1,), (1,)), ((), ())),
             preferred_element_type=jnp.float32,
         )
+
+    def weights_of(scores, live):
         scores = jnp.where(live, scores * scale, masked)
         top = jnp.maximum(jnp.max(scores, axis=1, keepdims=True), lowest)
         softmax_weights = jnp.exp2(scores - top)
         total = jnp.sum(softmax_weights, axis=1, keepdims=True)
         high = softmax_weights.astype(jnp.bfloat16)
         low = (softmax_weights - high.astype(jnp.float32)).astype(jnp.bfloat16)
-        weights[n, :group] = high
-        weights[n, group:] = low
-        tile = n // per_tile
-        mine = column == row + (n % per_tile) * group
-        tops[tile] = jnp.where(mine, top, tops[tile])
-        totals[tile] = jnp.where(mine, total, totals[tile])
-    for n in range(len(pairs)):
-        value_copies[n].wait()
-        both = lax.dot_general(
-            weights[n],
-            values[n],
-            (((1,), (0,)), ((), ())),
-            preferred_element_type=jnp.float32,
-        )
-        summed[n * group : (n + 1) * group, :] = both[:group] + both[group:]
+        return jnp.concatenate([high, low], axis=0), top, total
+
+    def summed_of(b, h, weights):
+        both = jnp.dot(weights, values[b, h], preferred_element_type=jnp.float32)
+        return both[:group] + both[group:]
+
+    per_tile = LANES // group
+    pairs = [(b, h) for b in range(batch_rows) for h in range(heads_local)]
+    tiles = len(pairs) // per_tile
+    row = lax.broadcasted_iota(jnp.int32, (group, LANES), 0)
+    column = lax.broadcasted_iota(jnp.int32, (group, LANES), 1)
+    tops = [jnp.zeros((group, LANES), jnp.float32) for _ in range(tiles)]
+    totals = [jnp.zeros((group, LANES), jnp.float32) for _ in range(tiles)]
+
+    def chunk_pairs(chunk):
+        size = rows * heads_local
+        return list(enumerate(pairs))[chunk * size : (chunk + 1) * size]
+
+    lives = [live_of(b, h) for b, h in pairs]
+    scores, weights, summed = {}, {}, {}
+    done_tiles = 0
+    for step in range(chunks + 2):
+        if step < chunks:
+            whole_of(step, *key_side).wait()
+        if step >= 2:
+            whole_of(step - 2, *value_side).wait()
+        if step < chunks:
+            for n, (b, h) in chunk_pairs(step):
+                scores[n] = scores_of(b, h)
+        if 1 <= step <= chunks:
+            for n, _ in chunk_pairs(step - 1):
+                weights[n], top, total = weights_of(scores.pop(n), lives[n])
+                tile = n // per_tile
+                mine = column == row + (n % per_tile) * group
+                tops[tile] = jnp.where(mine, top, tops[tile])
+                totals[tile] = jnp.where(mine, total, totals[tile])
+        if step >= 2:
+            for n, (b, h) in chunk_pairs(step - 2):
+                summed[n] = summed_of(b, h, weights.pop(n))
+        while all(done_tiles * per_tile + n in summed for n in range(per_tile)):
+            flipped[done_tiles] = jnp.concatenate(
+                [summed.pop(done_tiles * per_tile + n) for n in range(per_tile)], axis=0
+            ).T
+            done_tiles += 1
 
     stats = jnp.zeros((SUBLANES, LANES), jnp.float32)
     line = lax.broadcasted_iota(jnp.int32, (SUBLANES, LANES), 0)
     for tile in range(tiles):
         stats = jnp.where(line == tile, jnp.sum(tops[tile], axis=0, keepdims=True), stats)
         stats = jnp.where(line == tiles + tile, jnp.sum(totals[tile], axis=0, keepdims=True), stats)
-        flipped[tile] = summed[tile * LANES : (tile + 1) * LANES, :].T
 
     for s in range(seq_count):
         if relative:
@@ -188,9 +223,9 @@
     any_space = pl.BlockSpec(memory_space=pltpu.HBM)
     vmem = pl.BlockSpec(memory_space=pltpu.VMEM)
     if relative:
-        out_shape = [jax.ShapeDtypeStruct((piece_rows, LANES), jnp.float32)] * seq_count
+        out_shape = [pltpu.VMEM((piece_rows, LANES), jnp.float32)] * seq_count
     else:
-        out_shape = [jax.ShapeDtypeStruct((seq_count, piece_rows, LANES), jnp.float32)]
+        out_shape = [pltpu.VMEM((seq_count, piece_rows, LANES), jnp.float32)]
     pieces = pl.pallas_call(
         functools.partial(partial_kernel, seq_count, relative),
         out_shape=out_shape,
@@ -198,20 +233,24 @@
         out_specs=[vmem] * len(out_shape),
         scratch_shapes=[
             pltpu.VMEM(queries.shape, queries.dtype),
-            pltpu.VMEM((pairs, ctx_local, key_width), key_cache.dtype),
-            pltpu.VMEM((pairs, ctx_local, value_width), value_cache.dtype),
+            pltpu.VMEM(key_cache.shape, key_cache.dtype),
+            pltpu.VMEM(value_cache.shape, value_cache.dtype),
             pltpu.VMEM(indices.shape, indices.dtype),
             pltpu.SMEM((heads_local, batch_rows), counts.dtype),
             pltpu.SMEM(lengths.shape, lengths.dtype),
-            pltpu.VMEM((pairs, 2 * group, ctx_local), jnp.bfloat16),
-            pltpu.VMEM((pairs * group, value_width), jnp.float32),
             pltpu.VMEM((tiles, value_width, LANES), jnp.float32),
             pltpu.SemaphoreType.DMA((4,)),
-            pltpu.SemaphoreType.DMA((pairs,)),
-            pltpu.SemaphoreType.DMA((pairs,)),
+            pltpu.SemaphoreType.DMA((CHUNKS,)),
+            pltpu.SemaphoreType.DMA((CHUNKS,)),
         ],
+        compiler_params=pltpu.CompilerParams(vmem_limit_bytes=12 << 20),
         name="partial_attention",
-    )(queries, key_cache, value_cache, indices, counts.T, lengths)
+    )(
+        *(
+            pltpu.with_memory_space_constraint(operand, pltpu.HBM)
+            for operand in (queries, key_cache, value_cache, indices, counts.T, lengths)
+        )
+    )
     if relative:
         arrived = [pieces[0]] + [
             lax.ppermute(pieces[s], "seq", [(i, i ^ s) for i in range(seq_count)])
@@ -224,6 +263,7 @@
         out_shape=jax.ShapeDtypeStruct((batch_rows, heads, share), jnp.bfloat16),
         in_specs=[vmem] * len(arrived),
         out_specs=vmem,
+        compiler_params=pltpu.CompilerParams(vmem_limit_bytes=4 << 20),
         name="join_partials",
     )(*arrived)
 

time: 23.2 us -> 14.5 us (0.62)
  Pallas kernels: 12.2 us -> 4.37 us
  local copies, waits for them, and re-layouts: 0.62 us -> 0 us
    pallas_call x1, Pallas kernels: 10.6 us -> 3.61 us  [local(): pl.pallas_call(functools.partial(partial_kernel, seq_count, relative), ou...]
    pallas_call x1, Pallas kernels: 1.58 us -> 0.76 us  [local(): pl.pallas_call(functools.partial(join_kernel, tiles, share, group), out_s...]
    unnamed x6 -> x0, local copies, waits for them, and re-layouts: 0.62 us -> none
where the time goes in v2:
time: 14.5 us; the launch traced here: 14.4 us
  starting transfers between devices  5.79 us (40%)
  Pallas kernels  4.37 us (30%)
  waiting for transfers between devices  4.22 us (29%)
    ppermute x3, starting transfers between devices, local(): lax.ppermute(pieces[s], 'seq', [(i, i ^ s) for i in range(seq_count)])  5.79 us
    ppermute x3, waiting for transfers between devices, local(): lax.ppermute(pieces[s], 'seq', [(i, i ^ s) for i in range(seq_count)])  4.22 us
    pallas_call x1, Pallas kernels, local(): pl.pallas_call(functools.partial(partial_kernel, seq_count, relative), ou...  3.61 us
    pallas_call x1, Pallas kernels, local(): pl.pallas_call(functools.partial(join_kernel, tiles, share, group), out_s...  0.76 us
  transfers between devices with their start and end apart: 3, of which 2 were waited for; matrix products, arithmetic and copies ran while one was open for 0% of the time, Pallas kernels for 0%

profile of v2, /device:TPU:0, one launch (start us, length us, event | category | flops | bytes accessed | tf_op | source)
XLA Modules:
  0.0 14.4 jit_solution(6897092035591311823)
XLA Ops:
  0.0 3.6 %partial_attention.1 = (f32[72,128]{1,0:T(8,128)S(1)}, f32[72,128]{1,0:T(8,128)S(1)}, f32[72,128]{1,0:T(8,128)S(1)}, f32[72,128]{1,0:T(8,128)S(1)}) custom-call(bf16[8,32,128]{2,1,0:T(8,128)(2,1)} %queries_hbm.1, bf16[8,2,512,128]{3,2,1,0:T(8,128)(2,1)} %keys_hbm.1, bf16[8,2,512,128]{3,2,1,0:T(8,128)(2,1)} %values_hbm.1, s32[8,2,16]{2,1,0:T(2,128)} %indices_hbm.1, ...), custom_call_target="tpu_custom_call" | custom-call | tf_op jit(solution)/shard_map/partial_attention/pallas_call | solution.py:229
  3.6 5.1 %collective-permute-start = (f32[72,128]{1,0:T(8,128)S(1)}, f32[72,128]{1,0:T(8,128)S(1)}, u32[]{:S(2)}, u32[]{:S(2)}) collective-permute-start(f32[72,128]{1,0:T(8,128)S(1)} %get-tuple-element.10), channel_id=1, source_target_pairs={{0,12},{4,8},{8,4},{12,0},{1,13},{5,9},{9,5},{13,1},{2,14},{6,10},... | collective-permute-start | bytes 110600 | tf_op jit(solution)/shard_map/ppermute | solution.py:256
  8.8 0.0 collective-permute-start.1
  8.8 0.6 %collective-permute-start.2 = (f32[72,128]{1,0:T(8,128)S(1)}, f32[72,128]{1,0:T(8,128)S(1)}, u32[]{:S(2)}, u32[]{:S(2)}) collective-permute-start(f32[72,128]{1,0:T(8,128)S(1)} %get-tuple-element.12), channel_id=1, source_target_pairs={{0,4},{4,0},{8,12},{12,8},{1,5},{5,1},{9,13},{13,9},{2,6},{6,2},{1... | collective-permute-start | bytes 110600 | tf_op jit(solution)/shard_map/ppermute | solution.py:256
  9.4 1.3 %collective-permute-done.refs_1_ = f32[72,128]{1,0:T(8,128)S(1)} collective-permute-done((f32[72,128]{1,0:T(8,128)S(1)}, f32[72,128]{1,0:T(8,128)S(1)}, u32[]{:S(2)}, u32[]{:S(2)}) %collective-permute-start) | collective-permute-done | bytes 36896 | tf_op jit(solution)/shard_map/ppermute | solution.py:256
  10.7 2.9 %collective-permute-done.1.refs_2_ = f32[72,128]{1,0:T(8,128)S(1)} collective-permute-done((f32[72,128]{1,0:T(8,128)S(1)}, f32[72,128]{1,0:T(8,128)S(1)}, u32[]{:S(2)}, u32[]{:S(2)}) %collective-permute-start.1) | collective-permute-done | bytes 36896 | tf_op jit(solution)/shard_map/ppermute | solution.py:256
  13.6 0.0 collective-permute-done.2.refs_3_
  13.6 0.8 %join_partials.1 = bf16[8,32,32]{2,1,0:T(8,128)(2,1)} custom-call(f32[72,128]{1,0:T(8,128)S(1)} %get-tuple-element.9.refs_0_, f32[72,128]{1,0:T(8,128)S(1)} %collective-permute-done.refs_1_, f32[72,128]{1,0:T(8,128)S(1)} %collective-permute-done.1.refs_2_, f32[72,128]{1,0:T(8,128)S(1)} %collective-permute-done.2.refs_3_), custom_call_target="tpu_custom_call" | custom-call | tf_op jit(solution)/shard_map/join_partials/pallas_call | solution.py:261
Async XLA Ops:
  3.6 7.1 %collective-permute-start = (f32[72,128]{1,0:T(8,128)S(1)}, f32[72,128]{1,0:T(8,128)S(1)}, u32[]{:S(2)}, u32[]{:S(2)}) collective-permute-start(f32[72,128]{1,0:T(8,128)S(1)} %get-tuple-element.10), channel_id=1, source_target_pairs={{0,12},{4,8},{8,4},{12,0},{1,13},{5,9},{9,5},{13,1},{2,14},{6,10},... | collective-permute-start | bytes 110600 | tf_op jit(solution)/shard_map/ppermute | solution.py:256
  8.8 4.9 %collective-permute-start.1 = (f32[72,128]{1,0:T(8,128)S(1)}, f32[72,128]{1,0:T(8,128)S(1)}, u32[]{:S(2)}, u32[]{:S(2)}) collective-permute-start(f32[72,128]{1,0:T(8,128)S(1)} %get-tuple-element.11), channel_id=1, source_target_pairs={{0,8},{4,12},{8,0},{12,4},{1,9},{5,13},{9,1},{13,5},{2,10},{6,14},... | collective-permute-start | bytes 110600 | tf_op jit(solution)/shard_map/ppermute | solution.py:256
  8.8 4.9 %collective-permute-start.2 = (f32[72,128]{1,0:T(8,128)S(1)}, f32[72,128]{1,0:T(8,128)S(1)}, u32[]{:S(2)}, u32[]{:S(2)}) collective-permute-start(f32[72,128]{1,0:T(8,128)S(1)} %get-tuple-element.12), channel_id=1, source_target_pairs={{0,4},{4,0},{8,12},{12,8},{1,5},{5,1},{9,13},{13,9},{2,6},{6,2},{1... | collective-permute-start | bytes 110600 | tf_op jit(solution)/shard_map/ppermute | solution.py:256
